TPU v7x, 32 devices: a whole 2x2x4 slice. The times are simulated.
32 devices in a mesh: gx: 8 (over y, x, core), yz: 4 (over z).
Axes of the slice: x: 2, y: 2, z: 4, core: 2. Of those that a mesh axis runs over, the one named last changes fastest.
Arguments:
- vel: float32 [3, 48, 192, 1024], P(None, 'gx', 'yz'), may hold values from -6 to 6
- q_old: float32 [3, 48, 192, 1024], P(None, 'gx', None, 'yz'), may hold values from -6 to 6
- pressure_guess: float32 [48, 192, 1024], P('gx', None, 'yz'), may hold values from -6 to 6
- shear_shift: int32 [1], replicated, may hold values from 0 to 1023
Outputs:
- vel_next: float32 [3, 48, 192, 1024], P(None, 'gx', 'yz')
- q_next: float32 [3, 48, 192, 1024], P(None, 'gx', None, 'yz')
- pressure: float32 [48, 192, 1024], P('gx', None, 'yz')
All inputs are finite; a program needn't handle non-finite values.
Results may differ from a plain program's by a relative error of at most 0.00013.
Values sent between devices are 32-bit elements; how exact they have to be, the bound alone decides.
No kernel may reach another device: no remote copies, remote signals or barrier semaphores. Data moves between devices by JAX's collectives and lax.ppermute only.
A program may use at most 128 MiB of HBM per device.

v0:
```python
import math
import jax
import jax.numpy as jnp
from jax import lax
from jax.sharding import PartitionSpec as P

SWEEPS = 2
highest = lax.Precision.HIGHEST
viscosity = 0.05
time_step = 0.2
keep_weight = -5.0 / 9.0
section_weight = 15.0 / 16.0
shear_param = 1.5
fraction = 0.375


def padded_2(cells, sides, width):
    for axis, dim in sides:
        count = lax.axis_size(axis)
        head = lax.slice_in_dim(cells, 0, width, axis=dim)
        tail = lax.slice_in_dim(cells, cells.shape[dim] - width, cells.shape[dim], axis=dim)
        cells = jnp.concatenate(
            [
                lax.ppermute(tail, axis, [(i, (i + 1) % count) for i in range(count)]),
                cells,
                lax.ppermute(head, axis, [((i + 1) % count, i) for i in range(count)]),
            ],
            axis=dim,
        )
    return cells


def split_parts(packed, block_len):
    shaped = packed.reshape(packed.shape[:-1] + (packed.shape[-1] // (2 * block_len), 2, block_len))
    return (shaped[..., 0:1, :], shaped[..., 1:2, :])


def join_parts(real_part, imag_part, shape):
    return jnp.concatenate([real_part, imag_part], axis=-2).reshape(shape)


def turn(packed, wave, block_len):
    real_part, imag_part = split_parts(packed, block_len)
    return join_parts(-wave * imag_part, wave * real_part, packed.shape)


def scale_modes(packed, factor, block_len):
    real_part, imag_part = split_parts(packed, block_len)
    return join_parts(factor * real_part, factor * imag_part, packed.shape)


def rotate(packed, cosine, sine, block_len):
    real_part, imag_part = split_parts(packed, block_len)
    return join_parts(
        real_part * cosine - imag_part * sine, real_part * sine + imag_part * cosine, packed.shape
    )


def z_apply(packed, cos_z, sin_z, block_len, sign):
    with_cos = jnp.einsum("wz,nxzk->nxwk", cos_z, packed, precision=highest)
    with_sin = jnp.einsum("wz,nxzk->nxwk", sin_z, packed, precision=highest)
    real_part = with_cos[..., :block_len] + sign * with_sin[..., block_len:]
    imag_part = with_cos[..., block_len:] - sign * with_sin[..., :block_len]
    return jnp.concatenate([real_part, imag_part], axis=-1)


def x_slice(padded, offset, rows_x):
    return padded[:, 3 + offset : 3 + offset + rows_x]


def first_diff(padded, rows_x):
    return (
        45.0 * (x_slice(padded, 1, rows_x) - x_slice(padded, -1, rows_x))
        - 9.0 * (x_slice(padded, 2, rows_x) - x_slice(padded, -2, rows_x))
        + (x_slice(padded, 3, rows_x) - x_slice(padded, -3, rows_x))
    ) / 60.0


def second_diff(padded, rows_x):
    return (
        2.0 * (x_slice(padded, 3, rows_x) + x_slice(padded, -3, rows_x))
        - 27.0 * (x_slice(padded, 2, rows_x) + x_slice(padded, -2, rows_x))
        + 270.0 * (x_slice(padded, 1, rows_x) + x_slice(padded, -1, rows_x))
        - 490.0 * x_slice(padded, 0, rows_x)
    ) / 180.0


def local(vel, q_old, pressure_guess, shear_shift):
    rows_x = vel.shape[1]
    width_y = vel.shape[3]
    depth_z = q_old.shape[2]
    groups = lax.axis_size("yz")
    block_len = width_y // (2 * groups)
    group_id = lax.axis_index("yz")
    slab_id = lax.axis_index("gx")
    slabs = lax.axis_size("gx")
    total_x = rows_x * slabs
    offset = shear_shift[0]
    padded = padded_2(vel, (("gx", 1),), 3)
    tail_rows = padded[:, :3]
    front_rows = padded[:, rows_x + 3 :]
    moved_tail = (1.0 - fraction) * jnp.roll(tail_rows, -offset, axis=3) + fraction * jnp.roll(
        tail_rows, -offset - 1, axis=3
    )
    moved_front = (1.0 - fraction) * jnp.roll(front_rows, offset, axis=3) + fraction * jnp.roll(
        front_rows, offset + 1, axis=3
    )
    tail_rows = jnp.where(slab_id == 0, moved_tail, tail_rows)
    front_rows = jnp.where(slab_id == slabs - 1, moved_front, front_rows)
    padded = jnp.concatenate([tail_rows, vel, front_rows], axis=1)
    omega = 2.0 / total_x
    xpos = (
        (slab_id * rows_x + jnp.arange(rows_x, dtype=jnp.int32)).astype(jnp.float32)
        + 0.5
        - total_x / 2.0
    )
    background = (-shear_param * omega * xpos)[:, None, None]
    coriolis = jnp.stack(
        [2.0 * omega * vel[1], -(2.0 - shear_param) * omega * vel[0], jnp.zeros_like(vel[0])]
    )
    term_a = (
        -first_diff(padded * padded[0][None], rows_x)
        + viscosity * second_diff(padded, rows_x)
        + coriolis
    )
    term_b = -(vel[1] + background)[None] * vel
    term_c = -vel[2][None] * vel
    columns = jnp.arange(width_y, dtype=jnp.int32)
    part_id = columns // block_len % 2
    mode_col = columns // (2 * block_len) * block_len + columns % block_len
    angle_y = (
        2.0
        * math.pi
        / width_y
        * (columns[:, None] * mode_col[None, :] % width_y).astype(jnp.float32)
    )
    forward_y = jnp.where(part_id[None, :] == 0, jnp.cos(angle_y), -jnp.sin(angle_y)) / math.sqrt(
        width_y
    )

    def to_modes(field):
        flat = field.reshape(-1, width_y)
        return jnp.dot(
            flat, forward_y, precision=highest, preferred_element_type=jnp.float32
        ).reshape(field.shape)

    spec_a = to_modes(term_a)
    spec_b = to_modes(term_b)
    spec_c = to_modes(term_c)
    spec_u = to_modes(vel)
    cells_z = jnp.arange(depth_z, dtype=jnp.int32)
    angle_z = (
        2.0
        * math.pi
        / depth_z
        * (cells_z[:, None] * cells_z[None, :] % depth_z).astype(jnp.float32)
    )
    cos_z = jnp.cos(angle_z) / math.sqrt(depth_z)
    sin_z = jnp.sin(angle_z) / math.sqrt(depth_z)
    signed_z = jnp.where(cells_z < depth_z // 2, cells_z, cells_z - depth_z)
    wave_z = (2.0 * math.pi / depth_z * signed_z.astype(jnp.float32)).reshape(depth_z, 1, 1, 1)
    own_modes = group_id * block_len + jnp.arange(block_len, dtype=jnp.int32)
    own_wave = (2.0 * math.pi / width_y * own_modes.astype(jnp.float32)).reshape(1, 1, block_len)
    all_wave = (
        2.0
        * math.pi
        / width_y
        * jnp.arange(groups * block_len, dtype=jnp.int32).astype(jnp.float32)
    ).reshape(groups, 1, block_len)
    combined = (
        spec_a
        + turn(spec_b, all_wave, block_len)
        - viscosity * scale_modes(spec_u, all_wave * all_wave, block_len)
    )
    spectral = z_apply(
        lax.all_to_all(combined, "yz", split_axis=3, concat_axis=2, tiled=True),
        cos_z,
        sin_z,
        block_len,
        1.0,
    )
    spectral = spectral + turn(
        z_apply(
            lax.all_to_all(spec_c, "yz", split_axis=3, concat_axis=2, tiled=True),
            cos_z,
            sin_z,
            block_len,
            1.0,
        ),
        wave_z,
        block_len,
    )
    tendency = spectral - viscosity * scale_modes(
        z_apply(
            lax.all_to_all(spec_u, "yz", split_axis=3, concat_axis=2, tiled=True),
            cos_z,
            sin_z,
            block_len,
            1.0,
        ),
        wave_z * wave_z,
        block_len,
    )
    edge_angle = (
        2.0
        * math.pi
        / width_y
        * (
            (own_modes * offset % width_y).astype(jnp.float32)
            + fraction * own_modes.astype(jnp.float32)
        )
    )
    edge_cos = jnp.cos(edge_angle).reshape(1, 1, block_len)
    edge_sin = jnp.sin(edge_angle).reshape(1, 1, block_len)

    def fix_edges(stacked, depth_x):
        extent = stacked.shape[1]
        lower = stacked[:, :depth_x]
        upper = stacked[:, extent - depth_x :]
        middle = stacked[:, depth_x : extent - depth_x]
        lower = jnp.where(slab_id == 0, rotate(lower, edge_cos, edge_sin, block_len), lower)
        upper = jnp.where(
            slab_id == slabs - 1, rotate(upper, edge_cos, -edge_sin, block_len), upper
        )
        return jnp.concatenate([lower, middle, upper], axis=1)

    denom_half = (
        2.0
        + own_wave.reshape(1, block_len) * own_wave.reshape(1, block_len)
        + wave_z.reshape(depth_z, 1) * wave_z.reshape(depth_z, 1)
    )
    denom = jnp.concatenate([denom_half, denom_half], axis=-1)

    def faces(stacked):
        return fix_edges(padded_2(stacked, (("gx", 1),), 1), 1)

    first = faces(jnp.stack([tendency[0], pressure_guess]))
    along_x = first[0]
    press = first[1]
    diverge = (
        0.5 * (along_x[2:] - along_x[:-2])
        + turn(tendency[1], own_wave, block_len)
        + turn(tendency[2], wave_z, block_len)
    )
    for sweep_no in range(SWEEPS):
        if sweep_no > 0:
            press = faces(press[None])[0]
        press = (press[2:] + press[:-2] - diverge) / denom
    ghosted_p = faces(press[None])[0]
    slope_x = 0.5 * (ghosted_p[2:] - ghosted_p[:-2])
    gradient = jnp.stack(
        [slope_x, turn(press, own_wave, block_len), turn(press, wave_z, block_len)]
    )
    q_next = keep_weight * q_old + time_step * (tendency - gradient)
    spatial = z_apply(q_next, cos_z, sin_z, block_len, -1.0)
    weights = jnp.where(mode_col == 0, 1.0, 2.0).astype(jnp.float32)
    inverse_y = (
        jnp.where(part_id[:, None] == 0, jnp.cos(angle_y.T), -jnp.sin(angle_y.T))
        * weights[:, None]
        / math.sqrt(width_y)
    )
    piece = lax.all_to_all(spatial, "yz", split_axis=2, concat_axis=3, tiled=True)
    flat = piece.reshape(-1, width_y)
    correction = jnp.dot(
        flat, inverse_y, precision=highest, preferred_element_type=jnp.float32
    ).reshape(piece.shape)
    vel_next = vel + section_weight * correction
    return (vel_next, q_next, press)


def solution(mesh):
    placed = (P(None, "gx", "yz", None), P(None, "gx", None, "yz"), P("gx", None, "yz"), P())
    return jax.shard_map(
        local,
        mesh=mesh,
        in_specs=placed,
        out_specs=(P(None, "gx", "yz", None), P(None, "gx", None, "yz"), P("gx", None, "yz")),
        check_vma=False,
    )
```

profile of v0, /device:TPU:3, one launch (start us, length us, event | category | flops | bytes accessed | tf_op | source)
XLA Modules:
  0.0 829.1 jit_solution(1366526000127523778)
XLA Ops:
  0.7 4.5 slice_multiply_fusion.11
  6.0 29.1 %fusion.13 = f32[3,6,48,1024]{3,2,1,0:T(8,128)} fusion(s32[1024]{0:T(1024)S(1)} %fusion.193, pred[1024]{0:T(1024)(128)(4,1)S(1)} %fusion.190, f32[3,6,48,1024]{3,2,1,0:T(8,128)S(1)} %fusion.327), kind=kOutput, calls=%fused_computation.31 | convolution fusion | flops 10889461760 | bytes 7083008 | tf_op jit(solution)/shard_map/dot_general | solution.py:143
  35.1 8.8 %copy.33 = f32[3,6,48,1024]{2,1,0,3:T(8,128)} copy(f32[3,6,48,1024]{3,2,1,0:T(8,128)} %fusion.13) | data formatting | bytes 7077888 | tf_op jit(solution)/shard_map/dot_general | solution.py:143
  43.9 11.7 %reshape.517 = f32[4,1,221184]{2,1,0:T(1,128)} reshape(f32[1024,3,6,48]{3,2,1,0:T(8,128)} %bitcast.207) | data formatting | bytes 7077888
  55.6 4.7 all-to-all-start.1
  65.6 16.9 %select_multiply_fusion.6 = f32[1024,1024]{1,0:T(8,128)S(1)} fusion(s32[1024]{0:T(1024)S(1)} %fusion.193, pred[1024]{0:T(1024)(128)(4,1)S(1)} %fusion.190), kind=kLoop, calls=%fused_computation.50.clone.1.clone.1 | loop fusion | flops 17825792 | bytes 4199424 | tf_op jit(solution)/shard_map/dot_general | solution.py:143
  82.5 13.4 %fusion.104 = f32[1024,864]{0,1:T(8,128)} fusion(f32[864,1024]{1,0:T(8,128)S(1)} %bitcast.206, f32[1024,1024]{1,0:T(8,128)S(1)} %select_multiply_fusion.6), kind=kOutput, calls=%fused_computation.128 | convolution fusion | flops 10871635968 | bytes 11272192 | tf_op jit(solution)/shard_map/dot_general | solution.py:143
  96.0 5.8 reshape_reshape.2
  101.7 8.8 %copy.35 = f32[3,6,48,1024]{2,1,0,3:T(8,128)} copy(f32[3,6,48,1024]{3,2,1,0:T(8,128)} %bitcast.221) | data formatting | bytes 7077888 | tf_op jit(solution)/shard_map/reshape | solution.py:145
  110.5 11.7 %reshape.515 = f32[4,1,221184]{2,1,0:T(1,128)} reshape(f32[1024,3,6,48]{3,2,1,0:T(8,128)} %bitcast.208) | data formatting | bytes 7077888
  124.6 40.5 %fusion.11 = f32[3,6,48,4,2,128]{5,2,4,3,1,0:T(8,128)S(1)} fusion(s32[4,2,128]{2,1,0:T(2,128)S(1)} %fusion.195, pred[4,2,128]{2,1,0:T(4,128)(4,1)S(1)} %fusion.199, f32[3,6,48,1024,1,1]{3,2,5,4,1,0:T(8,128)S(1)} %fusion.325), kind=kOutput, calls=%fused_computation.29 | convolution fusion | flops 10889461760 | bytes 7083008 | tf_op jit(solution)/shard_map/dot_general | solution.py:143
  172.6 5.4 maximum_multiply_fusion
  178.0 5.0 all-to-all-start.2
  183.6 5.7 copy.30
  189.3 5.7 reshape.486
  194.9 5.6 mul.836
  216.0 8.3 fusion.331
  224.3 31.9 %add_subtract_fusion = f32[3,6,48,1024]{3,2,1,0:T(8,128)} fusion(f32[3,6,48,1024]{3,2,1,0:T(8,128)} %mul.836, f32[3,6,48,1024]{3,2,1,0:T(8,128)} %reshape.486, s32[1024]{0:T(1024)S(1)} %fusion.193, pred[1024]{0:T(1024)(128)(4,1)S(1)} %copy-done.33, f32[3,6,48,1024]{3,2,1,0:T(8,128)} %fusion.331), kind=kOutput, calls=%fused_computation.108 | convolution fusion | flops 10891231232 | bytes 14160896 | tf_op jit(solution)/shard_map/dot_general | solution.py:143
  256.3 8.8 %copy.31 = f32[3,6,48,1024]{2,1,0,3:T(8,128)} copy(f32[3,6,48,1024]{3,2,1,0:T(8,128)} %add_subtract_fusion) | data formatting | bytes 7077888 | tf_op jit(solution)/shard_map/sub | solution.py:171
  265.0 11.7 %reshape.519 = f32[4,1,221184]{2,1,0:T(1,128)} reshape(f32[1024,3,6,48]{3,2,1,0:T(8,128)} %bitcast.209) | data formatting | bytes 7077888
  276.7 5.2 all-to-all-start
  283.0 40.4 %reduce.1 = f32[4,221184]{1,0:T(4,128)} reduce(f32[4,1,221184]{2,1,0:T(1,128)} %all-to-all-done.1, f32[]{:T(128)} %broadcast.808), dimensions={1}, to_apply=%all_to_all.54.reduce_sub_computation | reduce | bytes 7077892 | tf_op jit(solution)/shard_map/all_to_all | solution.py:184
  323.4 14.8 %reshape.518 = f32[1024,3,6,48]{3,2,1,0:T(8,128)} reshape(f32[4,221184]{1,0:T(4,128)} %reduce.1) | data formatting | bytes 7077888
  338.2 8.7 %copy.34 = f32[3,6,48,4,256]{4,2,3,1,0:T(8,128)} copy(f32[3,6,48,4,256]{2,1,0,4,3:T(8,128)} %bitcast.210) | data formatting | bytes 7077888 | tf_op jit(solution)/shard_map/all_to_all | solution.py:184
  347.0 6.5 convolution_bitcast_fusion.4
  360.4 5.3 reshape.488
  365.8 6.6 slice_multiply_fusion.5
  372.3 5.0 pad_maximum_fusion.6
  377.4 5.6 reshape.489
  383.0 40.8 %reduce = f32[4,221184]{1,0:T(4,128)} reduce(f32[4,1,221184]{2,1,0:T(1,128)} %all-to-all-done.2, f32[]{:T(128)} %broadcast.808), dimensions={1}, to_apply=%all_to_all.58.reduce_sub_computation | reduce | bytes 7077892 | tf_op jit(solution)/shard_map/all_to_all | solution.py:195
  423.9 14.8 %reshape.516 = f32[1024,3,6,48]{3,2,1,0:T(8,128)} reshape(f32[4,221184]{1,0:T(4,128)} %reduce) | data formatting | bytes 7077888
  438.6 8.7 %copy.36 = f32[3,6,48,4,256]{4,2,3,1,0:T(8,128)} copy(f32[3,6,48,4,256]{2,1,0,4,3:T(8,128)} %bitcast.211) | data formatting | bytes 7077888 | tf_op jit(solution)/shard_map/all_to_all | solution.py:195
  447.4 6.5 convolution_bitcast_fusion.2
  460.8 5.3 reshape.491
  466.2 6.6 slice_multiply_fusion.3
  472.7 5.5 maximum_multiply_fusion.1
  478.2 5.6 mul.857
  483.8 40.8 %reduce.2 = f32[4,221184]{1,0:T(4,128)} reduce(f32[4,1,221184]{2,1,0:T(1,128)} %all-to-all-done, f32[]{:T(128)} %broadcast.808), dimensions={1}, to_apply=%all_to_all.50.reduce_sub_computation | reduce | bytes 7077892 | tf_op jit(solution)/shard_map/all_to_all | solution.py:176
  524.7 14.8 %reshape.520 = f32[1024,3,6,48]{3,2,1,0:T(8,128)} reshape(f32[4,221184]{1,0:T(4,128)} %reduce.2) | data formatting | bytes 7077888
  539.5 8.7 %copy.32 = f32[3,6,48,4,256]{4,2,3,1,0:T(8,128)} copy(f32[3,6,48,4,256]{2,1,0,4,3:T(8,128)} %bitcast.212) | data formatting | bytes 7077888 | tf_op jit(solution)/shard_map/all_to_all | solution.py:176
  548.2 6.5 convolution_bitcast_fusion.6
  689.0 4.5 copy.61
  693.6 5.1 all-to-all-start.3
  698.7 19.5 %fusion.329 = f32[1024,1024,1,1]{1,0,3,2:T(8,128)} fusion(f32[1024]{0:T(1024)S(1)} %compare_select_fusion.2, s32[1024]{0:T(1024)S(1)} %fusion.193, pred[1024]{0:T(1024)(128)(4,1)S(1)} %copy-done.34), kind=kLoop, calls=%fused_computation.28.clone.clone.clone.1 | loop fusion | flops 18874368 | bytes 4203520 | tf_op jit(solution)/shard_map/dot_general | solution.py:264
  718.2 83.7 %all-to-all-done.3 = f32[3,6,192,256]{3,1,0,2:T(8,128)} async-done(((f32[3,6,192,256]{3,1,0,2:T(8,128)}), f32[3,6,192,256]{3,1,0,2:T(8,128)}, u32[]{:S(2)}, u32[]{:S(2)}) %all-to-all-start.3) | async-done | bytes 3538976 | tf_op jit(solution)/shard_map/all_to_all | solution.py:262
  801.9 6.4 copy.88
  808.3 5.3 dot_general.56
  813.6 15.2 %multiply_add_fusion = f32[3,6,48,1024]{3,2,1,0:T(8,128)} fusion(f32[3,6,48,1024]{3,2,1,0:T(8,128)S(1)} %copy-done, f32[3,6,48,1024]{3,2,1,0:T(8,128)} %dot_general.56, f32[1024,1024,1,1]{1,0,3,2:T(8,128)} %fusion.329), kind=kOutput, calls=%fused_computation.106 | convolution fusion | flops 10873405440 | bytes 14811136 | tf_op jit(solution)/shard_map/dot_general | solution.py:264
  (202 shorter events, 180.0 us)
Async XLA Ops:
  0.7 65.0 %copy-start.32 = (pred[1024]{0:T(1024)(128)(4,1)}, pred[1024]{0:T(1024)(128)(4,1)S(1)}, u32[]{:S(2)}) copy-start(pred[1024]{0:T(1024)(128)(4,1)S(1)} %fusion.190) | copy-start | bytes 3076
  0.7 4.5 copy-start
  55.6 122.4 %all-to-all-start.1 = ((f32[4,1,221184]{2,1,0:T(1,128)}), f32[4,1,221184]{2,1,0:T(1,128)}, u32[]{:S(2)}, u32[]{:S(2)}) async-start(f32[4,1,221184]{2,1,0:T(1,128)} %reshape.517), calls=%async_computation.1 | async-start | bytes 7077888 | tf_op jit(solution)/shard_map/all_to_all | solution.py:184
  62.6 139.4 %collective-permute-start = (f32[3,3,48,1024]{3,2,1,0:T(8,128)}, f32[3,3,48,1024]{3,2,1,0:T(8,128)}, u32[]{:S(2)}, u32[]{:S(2)}) collective-permute-start(f32[3,3,48,1024]{3,2,1,0:T(8,128)} %get-tuple-element.30), channel_id=1, source_target_pairs={{0,4},{4,8},{8,12},{12,16},{16,20},{20,24},{24,28},{28,0},{1,5},{5... | collective-permute-start | bytes 5308424 | tf_op jit(solution)/shard_map/ppermute | solution.py:24
  64.5 140.9 %collective-permute-start.1 = (f32[3,3,48,1024]{3,2,1,0:T(8,128)}, f32[3,3,48,1024]{3,2,1,0:T(8,128)}, u32[]{:S(2)}, u32[]{:S(2)}) collective-permute-start(f32[3,3,48,1024]{3,2,1,0:T(8,128)} %get-tuple-element.29), channel_id=1, source_target_pairs={{4,0},{8,4},{12,8},{16,12},{20,16},{24,20},{28,24},{0,28},{5,1},{9... | collective-permute-start | bytes 5308424 | tf_op jit(solution)/shard_map/ppermute | solution.py:26
  165.6 3.3 copy-start.10
  178.0 98.7 %all-to-all-start.2 = ((f32[4,1,221184]{2,1,0:T(1,128)}), f32[4,1,221184]{2,1,0:T(1,128)}, u32[]{:S(2)}, u32[]{:S(2)}) async-start(f32[4,1,221184]{2,1,0:T(1,128)} %reshape.515), calls=%async_computation.2 | async-start | bytes 7077888 | tf_op jit(solution)/shard_map/all_to_all | solution.py:195
  216.0 8.3 %copy-start.33 = (pred[1024]{0:T(1024)(128)(4,1)S(1)}, pred[1024]{0:T(1024)(128)(4,1)}, u32[]{:S(2)}) copy-start(pred[1024]{0:T(1024)(128)(4,1)} %copy-done.32) | copy-start | bytes 3076
  276.7 207.1 %all-to-all-start = ((f32[4,1,221184]{2,1,0:T(1,128)}), f32[4,1,221184]{2,1,0:T(1,128)}, u32[]{:S(2)}, u32[]{:S(2)}) async-start(f32[4,1,221184]{2,1,0:T(1,128)} %reshape.519), calls=%async_computation | async-start | bytes 7077888 | tf_op jit(solution)/shard_map/all_to_all | solution.py:176
  347.0 6.5 copy-start.4
  447.4 6.5 copy-start.5
  548.2 6.5 copy-start.6
  559.1 2.0 copy-start.8
  559.1 3.1 copy-start.9
  562.9 2.5 copy-start.1
  562.9 3.6 copy-start.24
  565.4 1.0 copy-start.11
  567.4 28.1 %collective-permute-start.2 = (f32[2,1,192,256]{3,2,1,0:T(8,128)}, f32[2,1,192,256]{3,2,1,0:T(8,128)}, u32[]{:S(2)}, u32[]{:S(2)}) collective-permute-start(f32[2,1,192,256]{3,2,1,0:T(8,128)} %get-tuple-element.35), channel_id=1, source_target_pairs={{4,0},{8,4},{12,8},{16,12},{20,16},{24,20},{28,24},{0,28},{5,1},{9... | collective-permute-start | bytes 1179656 | tf_op jit(solution)/shard_map/ppermute | solution.py:26
  568.7 31.0 %collective-permute-start.3 = (f32[2,1,192,256]{3,2,1,0:T(8,128)}, f32[2,1,192,256]{3,2,1,0:T(8,128)}, u32[]{:S(2)}, u32[]{:S(2)}) collective-permute-start(f32[2,1,192,256]{3,2,1,0:T(8,128)} %get-tuple-element.36), channel_id=1, source_target_pairs={{0,4},{4,8},{8,12},{12,16},{16,20},{20,24},{24,28},{28,0},{1,5},{5... | collective-permute-start | bytes 1179656 | tf_op jit(solution)/shard_map/ppermute | solution.py:24
  603.1 4.1 copy-start.12
  603.1 4.1 copy-start.13
  603.2 4.1 copy-start.15
  603.2 4.1 copy-start.25
  603.2 4.1 copy-start.27
  607.3 3.3 copy-start.35
  608.8 1.0 copy-start.18
  610.6 13.1 %collective-permute-start.4 = (f32[1,1,192,256]{3,2,1,0:T(8,128)}, f32[1,1,192,256]{3,2,1,0:T(8,128)}, u32[]{:S(2)}, u32[]{:S(2)}) collective-permute-start(f32[1,1,192,256]{3,2,1,0:T(8,128)} %get-tuple-element.43), channel_id=1, source_target_pairs={{4,0},{8,4},{12,8},{16,12},{20,16},{24,20},{28,24},{0,28},{5,1},{9... | collective-permute-start | bytes 589832 | tf_op jit(solution)/shard_map/ppermute | solution.py:26
  615.2 15.1 %copy-start.29 = (f32[128]{0:T(128)S(1)}, f32[128]{0:T(128)}, u32[]{:S(2)}) copy-start(f32[128]{0:T(128)} %get-tuple-element.8) | copy-start | bytes 1540
  618.3 9.0 %collective-permute-start.5 = (f32[1,1,192,256]{3,2,1,0:T(8,128)}, f32[1,1,192,256]{3,2,1,0:T(8,128)}, u32[]{:S(2)}, u32[]{:S(2)}) collective-permute-start(f32[1,1,192,256]{3,2,1,0:T(8,128)} %get-tuple-element.44), channel_id=1, source_target_pairs={{0,4},{4,8},{8,12},{12,16},{16,20},{20,24},{24,28},{28,0},{1,5},{5... | collective-permute-start | bytes 589832 | tf_op jit(solution)/shard_map/ppermute | solution.py:24
  629.0 4.7 copy-start.7
  629.0 4.7 copy-start.19
  629.0 4.7 copy-start.26
  629.0 4.7 copy-start.28
  633.7 3.8 copy-start.14
  633.7 3.8 copy-start.16
  636.5 1.0 copy-start.17
  641.6 8.6 %copy-start.36 = (f32[128]{0:T(128)S(1)}, f32[128]{0:T(128)}, u32[]{:S(2)}) copy-start(f32[128]{0:T(128)} %get-tuple-element.85) | copy-start | bytes 1540
  641.6 8.6 %copy-start.37 = (f32[128]{0:T(128)S(1)}, f32[128]{0:T(128)}, u32[]{:S(2)}) copy-start(f32[128]{0:T(128)} %fusion.278) | copy-start | bytes 1540
  643.4 21.0 %collective-permute-start.6 = (f32[1,1,192,256]{3,2,1,0:T(8,128)}, f32[1,1,192,256]{3,2,1,0:T(8,128)}, u32[]{:S(2)}, u32[]{:S(2)}) collective-permute-start(f32[1,1,192,256]{3,2,1,0:T(8,128)} %get-tuple-element.37), channel_id=1, source_target_pairs={{4,0},{8,4},{12,8},{16,12},{20,16},{24,20},{28,24},{0,28},{5,1},{9... | collective-permute-start | bytes 589832 | tf_op jit(solution)/shard_map/ppermute | solution.py:26
  643.4 24.6 %collective-permute-start.7 = (f32[1,1,192,256]{3,2,1,0:T(8,128)}, f32[1,1,192,256]{3,2,1,0:T(8,128)}, u32[]{:S(2)}, u32[]{:S(2)}) collective-permute-start(f32[1,1,192,256]{3,2,1,0:T(8,128)} %get-tuple-element.38), channel_id=1, source_target_pairs={{0,4},{4,8},{8,12},{12,16},{16,20},{20,24},{24,28},{28,0},{1,5},{5... | collective-permute-start | bytes 589832 | tf_op jit(solution)/shard_map/ppermute | solution.py:24
  657.9 13.2 %copy-start.30 = (f32[128]{0:T(128)S(1)}, f32[128]{0:T(128)}, u32[]{:S(2)}) copy-start(f32[128]{0:T(128)} %get-tuple-element.9) | copy-start | bytes 1540
  657.9 13.2 %copy-start.31 = (f32[128]{0:T(128)S(1)}, f32[128]{0:T(128)}, u32[]{:S(2)}) copy-start(f32[128]{0:T(128)} %get-tuple-element.83) | copy-start | bytes 1540
  669.7 6.9 copy-start.2
  669.7 6.9 copy-start.22
  669.7 6.9 copy-start.23
  679.5 4.4 copy-start.3
  693.6 5.1 copy-start.34
  693.6 108.3 %all-to-all-start.3 = ((f32[3,6,192,256]{3,1,0,2:T(8,128)}), f32[3,6,192,256]{3,1,0,2:T(8,128)}, u32[]{:S(2)}, u32[]{:S(2)}) async-start(f32[3,6,192,256]{3,1,0,2:T(8,128)} %copy.61), calls=%async_computation.3 | async-start | bytes 9437184 | tf_op jit(solution)/shard_map/all_to_all | solution.py:262
  (2 other events, 1.8 us)
where the time goes:
time: 841 us; the launch traced here: 829 us
  other arithmetic  272 us (32%)
  local copies, waits for them, and re-layouts  268 us (32%)
  matrix products  172 us (20%)
  waiting for transfers between devices  83.7 us (10%)
  starting transfers between devices  30.9 us (4%)
    dot_general x4, matrix products, to_modes(): jnp.dot(flat, forward_y, precision=highest, preferred_element_type=jnp.fl...  115 us
    unnamed x84, local copies, waits for them, and re-layouts  91.6 us
    all_to_all x1, waiting for transfers between devices, local(): lax.all_to_all(spatial, 'yz', split_axis=2, concat_axis=3, tiled=True)  83.7 us
    all_to_all x1, other arithmetic, local(): lax.all_to_all(combined, 'yz', split_axis=3, concat_axis=2, tiled=True)  40.8 us
    all_to_all x1, other arithmetic, local(): lax.all_to_all(spec_u, 'yz', split_axis=3, concat_axis=2, tiled=True)  40.8 us
    all_to_all x1, other arithmetic, local(): lax.all_to_all(spec_c, 'yz', split_axis=3, concat_axis=2, tiled=True)  40.4 us
    dot_general x4, other arithmetic, to_modes(): jnp.dot(flat, forward_y, precision=highest, preferred_element_type=jnp.fl...  27.8 us
    reshape x6, local copies, waits for them, and re-layouts, join_parts(): return jnp.concatenate([real_part, imag_part], axis=-2).reshape(shape)  24.1 us
  transfers between devices with their start and end apart: 12, of which 1 were waited for; matrix products, arithmetic and copies ran while one was open for 59% of the time, Pallas kernels for 0%

commit v1 on v0

--- a/solution.py
+++ b/solution.py
@@ -259,7 +259,10 @@
         * weights[:, None]
         / math.sqrt(width_y)
     )
-    piece = lax.all_to_all(spatial, "yz", split_axis=2, concat_axis=3, tiled=True)
+    piece = jnp.concatenate(
+        lax.all_to_all(jnp.stack(jnp.split(spatial, lax.axis_size("yz"), axis=2)), "yz", 0, 0),
+        axis=3,
+    )
     flat = piece.reshape(-1, width_y)
     correction = jnp.dot(
         flat, inverse_y, precision=highest, preferred_element_type=jnp.float32

time: 841 us -> 803 us (0.955)
  waiting for transfers between devices: 83.7 us -> 58.6 us
  local copies, waits for them, and re-layouts: 268 us -> 256 us
    all_to_all x1, waiting for transfers between devices: 83.7 us -> 58.5 us  [local(): lax.all_to_all(jnp.stack(jnp.split(spatial, lax.axis_size('yz'), axis=2))...]
    unnamed x84 -> x86, local copies, waits for them, and re-layouts: 91.6 us -> 92.3 us
  transfers between devices with their start and end apart: 12 -> 12, of which waited for: 1 -> 1; matrix products, arithmetic and copies ran while one was open for 59% -> 62% of each run, Pallas kernels for 0% -> 0%
where the time goes in v1:
time: 803 us; the launch traced here: 792 us
  other arithmetic  274 us (34%)
  local copies, waits for them, and re-layouts  256 us (32%)
  matrix products  170 us (21%)
  waiting for transfers between devices  58.6 us (7%)
  starting transfers between devices  31 us (4%)
    dot_general x4, matrix products, to_modes(): jnp.dot(flat, forward_y, precision=highest, preferred_element_type=jnp.fl...  115 us
    unnamed x86, local copies, waits for them, and re-layouts  92.3 us
    all_to_all x1, waiting for transfers between devices, local(): lax.all_to_all(jnp.stack(jnp.split(spatial, lax.axis_size('yz'), axis=2))...  58.5 us
    all_to_all x1, other arithmetic, local(): lax.all_to_all(combined, 'yz', split_axis=3, concat_axis=2, tiled=True)  40.8 us
    all_to_all x1, other arithmetic, local(): lax.all_to_all(spec_u, 'yz', split_axis=3, concat_axis=2, tiled=True)  40.8 us
    all_to_all x1, other arithmetic, local(): lax.all_to_all(spec_c, 'yz', split_axis=3, concat_axis=2, tiled=True)  40.4 us
    dot_general x4, other arithmetic, to_modes(): jnp.dot(flat, forward_y, precision=highest, preferred_element_type=jnp.fl...  27.8 us
    reshape x6, local copies, waits for them, and re-layouts, join_parts(): return jnp.concatenate([real_part, imag_part], axis=-2).reshape(shape)  24.1 us
  transfers between devices with their start and end apart: 12, of which 1 were waited for; matrix products, arithmetic and copies ran while one was open for 62% of the time, Pallas kernels for 0%

profile of v1, /device:TPU:3, one launch (start us, length us, event | category | flops | bytes accessed | tf_op | source)
XLA Modules:
  0.0 791.7 jit_solution(9067445648968018792)
XLA Ops:
  0.7 4.5 slice_multiply_fusion.11
  6.0 29.1 %fusion.13 = f32[3,6,48,1024]{3,2,1,0:T(8,128)} fusion(s32[1024]{0:T(1024)S(1)} %fusion.200, pred[1024]{0:T(1024)(128)(4,1)S(1)} %fusion.197, f32[3,6,48,1024]{3,2,1,0:T(8,128)S(1)} %fusion.334), kind=kOutput, calls=%fused_computation.37 | convolution fusion | flops 10889461760 | bytes 7083008 | tf_op jit(solution)/shard_map/dot_general | solution.py:143
  35.1 9.0 %copy.35 = f32[3,6,48,1024]{2,1,0,3:T(8,128)} copy(f32[3,6,48,1024]{3,2,1,0:T(8,128)} %fusion.13) | data formatting | bytes 7077888 | tf_op jit(solution)/shard_map/dot_general | solution.py:143
  44.1 11.7 %reshape.519 = f32[4,1,221184]{2,1,0:T(1,128)} reshape(f32[1024,3,6,48]{3,2,1,0:T(8,128)} %bitcast.214) | data formatting | bytes 7077888
  55.8 4.7 all-to-all-start.1
  65.8 16.9 %select_multiply_fusion.6 = f32[1024,1024]{1,0:T(8,128)S(1)} fusion(s32[1024]{0:T(1024)S(1)} %fusion.200, pred[1024]{0:T(1024)(128)(4,1)S(1)} %fusion.197), kind=kLoop, calls=%fused_computation.56.clone.1.clone.1 | loop fusion | flops 17825792 | bytes 4199424 | tf_op jit(solution)/shard_map/dot_general | solution.py:143
  82.7 13.4 %fusion.104 = f32[1024,864]{0,1:T(8,128)} fusion(f32[864,1024]{1,0:T(8,128)S(1)} %bitcast.213, f32[1024,1024]{1,0:T(8,128)S(1)} %select_multiply_fusion.6), kind=kOutput, calls=%fused_computation.133 | convolution fusion | flops 10871635968 | bytes 11272192 | tf_op jit(solution)/shard_map/dot_general | solution.py:143
  96.1 5.8 reshape_reshape.2
  101.9 9.0 %copy.37 = f32[3,6,48,1024]{2,1,0,3:T(8,128)} copy(f32[3,6,48,1024]{3,2,1,0:T(8,128)} %bitcast.228) | data formatting | bytes 7077888 | tf_op jit(solution)/shard_map/reshape | solution.py:145
  110.9 11.7 %reshape.517 = f32[4,1,221184]{2,1,0:T(1,128)} reshape(f32[1024,3,6,48]{3,2,1,0:T(8,128)} %bitcast.215) | data formatting | bytes 7077888
  125.0 40.5 %fusion.11 = f32[3,6,48,4,2,128]{5,2,4,3,1,0:T(8,128)S(1)} fusion(s32[4,2,128]{2,1,0:T(2,128)S(1)} %fusion.202, pred[4,2,128]{2,1,0:T(4,128)(4,1)S(1)} %fusion.206, f32[3,6,48,1024,1,1]{3,2,5,4,1,0:T(8,128)S(1)} %fusion.332), kind=kOutput, calls=%fused_computation.35 | convolution fusion | flops 10889461760 | bytes 7083008 | tf_op jit(solution)/shard_map/dot_general | solution.py:143
  172.9 5.4 maximum_multiply_fusion
  178.4 5.0 all-to-all-start.2
  184.0 5.7 copy.32
  189.6 5.7 reshape.487
  195.3 5.6 mul.836
  216.4 8.3 %fusion.338 = f32[3,6,48,1024]{3,2,1,0:T(8,128)} fusion(f32[3,6,48,1024]{3,2,1,0:T(8,128)S(1)} %copy-done, f32[3,3,48,1024]{3,2,1,0:T(8,128)S(1)} %fusion.117, f32[3,3,48,1024]{3,2,1,0:T(8,128)S(1)} %fusion.115, f32[3,12,48,1024]{3,2,1,0:T(8,128)S(1)} %broadcast_multiply_fusion, f32[1,6,48,1024]{3,2,1,0:T(8,128)} %get-tuple-element.31, ...), kind=kLoop, calls=%fused_computation.70.clone.clone.clone.clone.2 | loop fusion | flops 26542080 | bytes 34209804 | tf_op jit(solution)/shard_map/dot_general | solution.py:143
  224.8 31.9 %add_subtract_fusion = f32[3,6,48,1024]{3,2,1,0:T(8,128)} fusion(f32[3,6,48,1024]{3,2,1,0:T(8,128)} %mul.836, f32[3,6,48,1024]{3,2,1,0:T(8,128)} %reshape.487, s32[1024]{0:T(1024)S(1)} %fusion.200, pred[1024]{0:T(1024)(128)(4,1)S(1)} %copy-done.34, f32[3,6,48,1024]{3,2,1,0:T(8,128)} %fusion.338), kind=kOutput, calls=%fused_computation.113 | convolution fusion | flops 10891231232 | bytes 14160896 | tf_op jit(solution)/shard_map/dot_general | solution.py:143
  256.7 9.0 %copy.33 = f32[3,6,48,1024]{2,1,0,3:T(8,128)} copy(f32[3,6,48,1024]{3,2,1,0:T(8,128)} %add_subtract_fusion) | data formatting | bytes 7077888 | tf_op jit(solution)/shard_map/sub | solution.py:171
  265.7 11.7 %reshape.521 = f32[4,1,221184]{2,1,0:T(1,128)} reshape(f32[1024,3,6,48]{3,2,1,0:T(8,128)} %bitcast.216) | data formatting | bytes 7077888
  277.3 5.2 all-to-all-start
  283.6 40.4 %reduce.1 = f32[4,221184]{1,0:T(4,128)} reduce(f32[4,1,221184]{2,1,0:T(1,128)} %all-to-all-done.1, f32[]{:T(128)} %broadcast.808), dimensions={1}, to_apply=%all_to_all.46.reduce_sub_computation | reduce | bytes 7077892 | tf_op jit(solution)/shard_map/all_to_all | solution.py:184
  324.0 14.8 %reshape.520 = f32[1024,3,6,48]{3,2,1,0:T(8,128)} reshape(f32[4,221184]{1,0:T(4,128)} %reduce.1) | data formatting | bytes 7077888
  338.8 8.7 %copy.36 = f32[3,6,48,4,256]{4,2,3,1,0:T(8,128)} copy(f32[3,6,48,4,256]{2,1,0,4,3:T(8,128)} %bitcast.217) | data formatting | bytes 7077888 | tf_op jit(solution)/shard_map/all_to_all | solution.py:184
  347.6 6.5 convolution_bitcast_fusion.4
  354.1 4.4 convolution_bitcast_fusion.5
  361.0 5.3 reshape.489
  366.3 6.6 slice_multiply_fusion.5
  372.9 5.0 pad_maximum_fusion.6
  378.0 5.6 reshape.490
  383.6 40.8 %reduce = f32[4,221184]{1,0:T(4,128)} reduce(f32[4,1,221184]{2,1,0:T(1,128)} %all-to-all-done.2, f32[]{:T(128)} %broadcast.808), dimensions={1}, to_apply=%all_to_all.50.reduce_sub_computation | reduce | bytes 7077892 | tf_op jit(solution)/shard_map/all_to_all | solution.py:195
  424.4 14.8 %reshape.518 = f32[1024,3,6,48]{3,2,1,0:T(8,128)} reshape(f32[4,221184]{1,0:T(4,128)} %reduce) | data formatting | bytes 7077888
  439.2 8.7 %copy.38 = f32[3,6,48,4,256]{4,2,3,1,0:T(8,128)} copy(f32[3,6,48,4,256]{2,1,0,4,3:T(8,128)} %bitcast.218) | data formatting | bytes 7077888 | tf_op jit(solution)/shard_map/all_to_all | solution.py:195
  448.0 6.5 convolution_bitcast_fusion.2
  454.5 4.4 convolution_bitcast_fusion.3
  461.4 5.3 reshape.492
  466.8 6.6 slice_multiply_fusion.3
  473.3 5.5 maximum_multiply_fusion.1
  478.8 5.6 mul.857
  484.4 40.8 %reduce.2 = f32[4,221184]{1,0:T(4,128)} reduce(f32[4,1,221184]{2,1,0:T(1,128)} %all-to-all-done, f32[]{:T(128)} %broadcast.808), dimensions={1}, to_apply=%all_to_all.42.reduce_sub_computation | reduce | bytes 7077892 | tf_op jit(solution)/shard_map/all_to_all | solution.py:176
  525.3 14.8 %reshape.522 = f32[1024,3,6,48]{3,2,1,0:T(8,128)} reshape(f32[4,221184]{1,0:T(4,128)} %reduce.2) | data formatting | bytes 7077888
  540.1 8.7 %copy.34 = f32[3,6,48,4,256]{4,2,3,1,0:T(8,128)} copy(f32[3,6,48,4,256]{2,1,0,4,3:T(8,128)} %bitcast.219) | data formatting | bytes 7077888 | tf_op jit(solution)/shard_map/all_to_all | solution.py:176
  548.8 6.5 convolution_bitcast_fusion.6
  680.1 4.4 convolution_bitcast_fusion
  691.7 5.2 all-to-all-start.3
  696.9 19.5 %fusion.336 = f32[1024,1024,1,1]{1,0,3,2:T(8,128)} fusion(f32[1024]{0:T(1024)S(1)} %compare_select_fusion.2, s32[1024]{0:T(1024)S(1)} %fusion.200, pred[1024]{0:T(1024)(128)(4,1)S(1)} %copy-done.35), kind=kLoop, calls=%fused_computation.34.clone.clone.clone.1 | loop fusion | flops 18874368 | bytes 4203520 | tf_op jit(solution)/shard_map/dot_general | solution.py:267
  716.4 58.5 %all-to-all-done.3 = f32[4,3,6,48,256]{4,3,2,1,0:T(8,128)} async-done(((f32[4,3,6,48,256]{4,3,2,1,0:T(8,128)}), f32[4,3,6,48,256]{4,3,2,1,0:T(8,128)}, u32[]{:S(2)}, u32[]{:S(2)}) %all-to-all-start.3) | async-done | bytes 3538976 | tf_op jit(solution)/shard_map/all_to_all | solution.py:263
  778.2 13.3 %multiply_add_fusion = f32[3,6,48,1024]{3,2,1,0:T(8,128)} fusion(f32[3,6,48,1024]{3,2,1,0:T(8,128)S(1)} %copy-done, f32[3,6,48,1024]{3,2,1,0:T(8,128)S(1)} %bitcast.226, f32[1024,1024,1,1]{1,0,3,2:T(8,128)S(1)} %copy-done.8), kind=kOutput, calls=%fused_computation.111 | convolution fusion | flops 10873405440 | bytes 14811136 | tf_op jit(solution)/shard_map/dot_general | solution.py:267
  (203 shorter events, 172.1 us)
Async XLA Ops:
  0.7 65.1 %copy-start.33 = (pred[1024]{0:T(1024)(128)(4,1)}, pred[1024]{0:T(1024)(128)(4,1)S(1)}, u32[]{:S(2)}) copy-start(pred[1024]{0:T(1024)(128)(4,1)S(1)} %fusion.197) | copy-start | bytes 3076
  0.7 4.5 copy-start
  55.8 122.6 %all-to-all-start.1 = ((f32[4,1,221184]{2,1,0:T(1,128)}), f32[4,1,221184]{2,1,0:T(1,128)}, u32[]{:S(2)}, u32[]{:S(2)}) async-start(f32[4,1,221184]{2,1,0:T(1,128)} %reshape.519), calls=%async_computation.1 | async-start | bytes 7077888 | tf_op jit(solution)/shard_map/all_to_all | solution.py:184
  62.8 139.6 %collective-permute-start = (f32[3,3,48,1024]{3,2,1,0:T(8,128)}, f32[3,3,48,1024]{3,2,1,0:T(8,128)}, u32[]{:S(2)}, u32[]{:S(2)}) collective-permute-start(f32[3,3,48,1024]{3,2,1,0:T(8,128)} %get-tuple-element.34), channel_id=1, source_target_pairs={{0,4},{4,8},{8,12},{12,16},{16,20},{20,24},{24,28},{28,0},{1,5},{5... | collective-permute-start | bytes 5308424 | tf_op jit(solution)/shard_map/ppermute | solution.py:24
  64.7 141.1 %collective-permute-start.1 = (f32[3,3,48,1024]{3,2,1,0:T(8,128)}, f32[3,3,48,1024]{3,2,1,0:T(8,128)}, u32[]{:S(2)}, u32[]{:S(2)}) collective-permute-start(f32[3,3,48,1024]{3,2,1,0:T(8,128)} %get-tuple-element.33), channel_id=1, source_target_pairs={{4,0},{8,4},{12,8},{16,12},{20,16},{24,20},{28,24},{0,28},{5,1},{9... | collective-permute-start | bytes 5308424 | tf_op jit(solution)/shard_map/ppermute | solution.py:26
  166.0 3.3 copy-start.11
  178.4 99.0 %all-to-all-start.2 = ((f32[4,1,221184]{2,1,0:T(1,128)}), f32[4,1,221184]{2,1,0:T(1,128)}, u32[]{:S(2)}, u32[]{:S(2)}) async-start(f32[4,1,221184]{2,1,0:T(1,128)} %reshape.517), calls=%async_computation.2 | async-start | bytes 7077888 | tf_op jit(solution)/shard_map/all_to_all | solution.py:195
  216.4 8.3 %copy-start.34 = (pred[1024]{0:T(1024)(128)(4,1)S(1)}, pred[1024]{0:T(1024)(128)(4,1)}, u32[]{:S(2)}) copy-start(pred[1024]{0:T(1024)(128)(4,1)} %copy-done.33) | copy-start | bytes 3076
  277.3 207.1 %all-to-all-start = ((f32[4,1,221184]{2,1,0:T(1,128)}), f32[4,1,221184]{2,1,0:T(1,128)}, u32[]{:S(2)}, u32[]{:S(2)}) async-start(f32[4,1,221184]{2,1,0:T(1,128)} %reshape.521), calls=%async_computation | async-start | bytes 7077888 | tf_op jit(solution)/shard_map/all_to_all | solution.py:176
  347.6 6.5 copy-start.4
  448.0 6.5 copy-start.5
  548.8 6.5 copy-start.6
  559.7 2.0 copy-start.9
  559.7 3.1 copy-start.10
  563.5 2.5 copy-start.1
  563.5 3.6 copy-start.25
  566.1 1.0 copy-start.12
  568.0 28.1 %collective-permute-start.2 = (f32[2,1,192,256]{3,2,1,0:T(8,128)}, f32[2,1,192,256]{3,2,1,0:T(8,128)}, u32[]{:S(2)}, u32[]{:S(2)}) collective-permute-start(f32[2,1,192,256]{3,2,1,0:T(8,128)} %get-tuple-element.39), channel_id=1, source_target_pairs={{4,0},{8,4},{12,8},{16,12},{20,16},{24,20},{28,24},{0,28},{5,1},{9... | collective-permute-start | bytes 1179656 | tf_op jit(solution)/shard_map/ppermute | solution.py:26
  569.3 31.0 %collective-permute-start.3 = (f32[2,1,192,256]{3,2,1,0:T(8,128)}, f32[2,1,192,256]{3,2,1,0:T(8,128)}, u32[]{:S(2)}, u32[]{:S(2)}) collective-permute-start(f32[2,1,192,256]{3,2,1,0:T(8,128)} %get-tuple-element.40), channel_id=1, source_target_pairs={{0,4},{4,8},{8,12},{12,16},{16,20},{20,24},{24,28},{28,0},{1,5},{5... | collective-permute-start | bytes 1179656 | tf_op jit(solution)/shard_map/ppermute | solution.py:24
  603.7 4.1 copy-start.13
  603.7 4.1 copy-start.14
  603.7 4.1 copy-start.16
  603.7 4.1 copy-start.26
  603.7 4.1 copy-start.28
  607.9 3.3 copy-start.36
  609.3 1.0 copy-start.19
  611.2 13.1 %collective-permute-start.4 = (f32[1,1,192,256]{3,2,1,0:T(8,128)}, f32[1,1,192,256]{3,2,1,0:T(8,128)}, u32[]{:S(2)}, u32[]{:S(2)}) collective-permute-start(f32[1,1,192,256]{3,2,1,0:T(8,128)} %get-tuple-element.47), channel_id=1, source_target_pairs={{4,0},{8,4},{12,8},{16,12},{20,16},{24,20},{28,24},{0,28},{5,1},{9... | collective-permute-start | bytes 589832 | tf_op jit(solution)/shard_map/ppermute | solution.py:26
  615.8 15.1 %copy-start.30 = (f32[128]{0:T(128)S(1)}, f32[128]{0:T(128)}, u32[]{:S(2)}) copy-start(f32[128]{0:T(128)} %get-tuple-element.8) | copy-start | bytes 1540
  618.8 9.0 %collective-permute-start.5 = (f32[1,1,192,256]{3,2,1,0:T(8,128)}, f32[1,1,192,256]{3,2,1,0:T(8,128)}, u32[]{:S(2)}, u32[]{:S(2)}) collective-permute-start(f32[1,1,192,256]{3,2,1,0:T(8,128)} %get-tuple-element.48), channel_id=1, source_target_pairs={{0,4},{4,8},{8,12},{12,16},{16,20},{20,24},{24,28},{28,0},{1,5},{5... | collective-permute-start | bytes 589832 | tf_op jit(solution)/shard_map/ppermute | solution.py:24
  629.5 4.7 copy-start.7
  629.5 4.7 copy-start.20
  629.5 4.7 copy-start.27
  629.5 4.7 copy-start.29
  634.2 3.8 copy-start.15
  634.2 3.8 copy-start.17
  642.2 8.6 %copy-start.37 = (f32[128]{0:T(128)S(1)}, f32[128]{0:T(128)}, u32[]{:S(2)}) copy-start(f32[128]{0:T(128)} %get-tuple-element.89) | copy-start | bytes 1540
  642.2 8.6 %copy-start.38 = (f32[128]{0:T(128)S(1)}, f32[128]{0:T(128)}, u32[]{:S(2)}) copy-start(f32[128]{0:T(128)} %fusion.285) | copy-start | bytes 1540
  644.0 21.0 %collective-permute-start.6 = (f32[1,1,192,256]{3,2,1,0:T(8,128)}, f32[1,1,192,256]{3,2,1,0:T(8,128)}, u32[]{:S(2)}, u32[]{:S(2)}) collective-permute-start(f32[1,1,192,256]{3,2,1,0:T(8,128)} %get-tuple-element.41), channel_id=1, source_target_pairs={{4,0},{8,4},{12,8},{16,12},{20,16},{24,20},{28,24},{0,28},{5,1},{9... | collective-permute-start | bytes 589832 | tf_op jit(solution)/shard_map/ppermute | solution.py:26
  644.0 24.6 %collective-permute-start.7 = (f32[1,1,192,256]{3,2,1,0:T(8,128)}, f32[1,1,192,256]{3,2,1,0:T(8,128)}, u32[]{:S(2)}, u32[]{:S(2)}) collective-permute-start(f32[1,1,192,256]{3,2,1,0:T(8,128)} %get-tuple-element.42), channel_id=1, source_target_pairs={{0,4},{4,8},{8,12},{12,16},{16,20},{20,24},{24,28},{28,0},{1,5},{5... | collective-permute-start | bytes 589832 | tf_op jit(solution)/shard_map/ppermute | solution.py:24
  658.5 13.2 %copy-start.31 = (f32[128]{0:T(128)S(1)}, f32[128]{0:T(128)}, u32[]{:S(2)}) copy-start(f32[128]{0:T(128)} %get-tuple-element.9) | copy-start | bytes 1540
  658.5 13.2 %copy-start.32 = (f32[128]{0:T(128)S(1)}, f32[128]{0:T(128)}, u32[]{:S(2)}) copy-start(f32[128]{0:T(128)} %get-tuple-element.87) | copy-start | bytes 1540
  670.3 6.9 copy-start.2
  670.3 6.9 copy-start.23
  670.3 6.9 copy-start.24
  680.1 4.4 copy-start.3
  691.7 5.2 copy-start.35
  691.7 83.2 %all-to-all-start.3 = ((f32[4,3,6,48,256]{4,3,2,1,0:T(8,128)}), f32[4,3,6,48,256]{4,3,2,1,0:T(8,128)}, u32[]{:S(2)}, u32[]{:S(2)}) async-start(f32[4,3,6,48,256]{4,3,2,1,0:T(8,128)} %pad_maximum_fusion.8), calls=%async_computation.3 | async-start | bytes 7077888 | tf_op jit(solution)/shard_map/all_to_all | solution.py:263
  774.9 3.3 copy-start.8
  (3 other events, 2.8 us)
